TPU v7x, 32 devices: a whole 2x2x4 slice. The times are simulated.
32 devices in a mesh: blk: 4 (over y, x), grp: 8 (over z, core).
Axes of the slice: x: 2, y: 2, z: 4, core: 2. Of those that a mesh axis runs over, the one named last changes fastest.
Arguments:
- queries: bfloat16 [32, 32, 128], P('blk', 'grp'), may hold values from -3 to 3
- token_counts: int32 [32], P('blk'), may hold values from 8 to 32
- pages: bfloat16 [32, 1024, 128], P(('blk', 'grp')), may hold values from -6 to 6
- patch_counts: int32 [32], P(('blk', 'grp')), may hold values from 512 to 1024
- labels: int32 [32, 32], P(None, ('blk', 'grp')), may hold values 0 or 1
Outputs:
- query_grad: float32 [32, 32, 128], P('blk', 'grp')
- page_grad: float32 [32, 1024, 128], P(('blk', 'grp'))
- page_loss: float32 [32], P(('blk', 'grp'))
All inputs are finite; a program needn't handle non-finite values. No bound on the sum of `labels` on one device may be relied on, other than what follows from the above.
Results may differ from a plain program's by a relative error of at most 0.018.
Values may be sent and summed in bfloat16 or wider, within the bound.
A program may use at most 64 MiB of HBM per device.

v0:
```python
import jax
import jax.numpy as jnp
from jax import lax
from jax.sharding import PartitionSpec as P

align_sharpness = 4.0
logit_scale = 2.0
logit_bias = -5.0


def align(query_rows, counts, page_rows, patch_count, label_column):
    query_number = counts.shape[0]
    token_slots = query_rows.shape[0] // query_number
    scores = jnp.dot(query_rows, page_rows.T, preferred_element_type=jnp.float32)
    patch_mask = jnp.arange(page_rows.shape[0]) < patch_count
    logits = jnp.where(patch_mask[None, :], align_sharpness * scores, -jnp.inf)
    row_max = jnp.max(logits, axis=1, keepdims=True)
    exponent = jnp.exp(logits - row_max)
    weights = exponent / jnp.sum(exponent, axis=1, keepdims=True)
    token_score = jnp.sum(weights * scores, axis=1)
    token_mask = jnp.arange(token_slots)[None, :] < counts[:, None]
    count_float = counts.astype(jnp.float32)
    pair_score = (
        jnp.sum(
            jnp.where(token_mask, token_score.reshape(query_number, token_slots), jnp.float32(0.0)),
            axis=1,
        )
        / count_float
    )
    label_sign = 2.0 * label_column.astype(jnp.float32) - 1.0
    pair_logit = logit_scale * pair_score + logit_bias
    loss_sum = jnp.sum(jax.nn.softplus(-label_sign * pair_logit))
    score_grad = -label_sign * logit_scale * jax.nn.sigmoid(-label_sign * pair_logit)
    token_grad = jnp.where(
        token_mask, (score_grad / count_float)[:, None], jnp.float32(0.0)
    ).reshape(-1)
    scores_grad = (
        token_grad[:, None] * weights * (1.0 + align_sharpness * (scores - token_score[:, None]))
    ).astype(jnp.bfloat16)
    query_term = jnp.dot(scores_grad, page_rows, preferred_element_type=jnp.float32)
    page_term = jnp.dot(scores_grad.T, query_rows, preferred_element_type=jnp.float32)
    return (query_term, page_term, loss_sum)


def local(queries, token_counts, pages, patch_counts, labels):
    page_rows = pages[0]
    patch_count = patch_counts[0]
    label_column = labels[:, 0]
    feature_width = page_rows.shape[1]
    blocks = lax.axis_size("blk")
    groups = lax.axis_size("grp")
    block_queries = token_counts.shape[0]
    gathered = lax.all_gather(queries, "grp", axis=1, tiled=True)
    query_tokens = gathered.shape[1]
    total_queries = block_queries * blocks
    empty_page = jnp.zeros(page_rows.shape, jnp.float32)

    def block_terms(held_queries, held_counts, source):
        labels_here = lax.dynamic_slice_in_dim(label_column, source * block_queries, block_queries)
        return align(
            held_queries.reshape(-1, feature_width),
            held_counts,
            page_rows,
            patch_count,
            labels_here,
        )

    slice_tokens = query_tokens // groups
    buffer = jnp.zeros((blocks * groups * block_queries, slice_tokens, feature_width), jnp.float32)
    piece_queries = lax.all_gather(gathered, "blk", axis=0, tiled=True)
    piece_counts = lax.all_gather(token_counts, "blk", axis=0, tiled=True)
    count_blocks = piece_queries.shape[0] // block_queries

    def one_block(inner_index, state_in):
        page_grad, loss_sum, collected = state_in
        held_queries = lax.dynamic_slice_in_dim(
            piece_queries, inner_index * block_queries, block_queries
        )
        held_counts = lax.dynamic_slice_in_dim(
            piece_counts, inner_index * block_queries, block_queries
        )
        query_term, page_term, loss_term = block_terms(held_queries, held_counts, inner_index)
        arranged = query_term.reshape(block_queries, groups, slice_tokens, feature_width)
        arranged = arranged.transpose(1, 0, 2, 3).reshape(
            groups * block_queries, slice_tokens, feature_width
        )
        collected = lax.dynamic_update_slice_in_dim(
            collected, arranged, inner_index * groups * block_queries, 0
        )
        return (page_grad + page_term, loss_sum + loss_term, collected)

    page_grad, loss_sum, buffer = lax.fori_loop(
        0, count_blocks, one_block, (empty_page, jnp.float32(0.0), buffer)
    )
    query_grad = lax.psum_scatter(buffer, ("blk", "grp"), scatter_dimension=0, tiled=True)
    page_loss = (loss_sum / jnp.float32(total_queries)).reshape(1)
    return (query_grad, page_grad[None], page_loss)


def solution(mesh):
    in_specs = (
        P("blk", "grp", None),
        P("blk"),
        P(("blk", "grp"), None, None),
        P(("blk", "grp")),
        P(None, ("blk", "grp")),
    )
    out_specs = (P("blk", "grp", None), P(("blk", "grp"), None, None), P(("blk", "grp")))
    return jax.shard_map(local, mesh=mesh, in_specs=in_specs, out_specs=out_specs, check_vma=False)
```

profile of v0, /device:TPU:0, one launch (start us, length us, event | category | flops | bytes accessed | tf_op | source)
XLA Modules:
  0.0 203.5 jit_solution(7265506860128643885)
XLA Ops:
  7.2 0.7 copy.13
  7.9 15.7 %all_gather.10 = bf16[8,32,128]{2,0,1:T(8,128)(2,1)S(1)} all-gather(bf16[8,4,128]{2,0,1:T(8,128)(2,1)S(1)} %copy.13), channel_id=1, replica_groups=mesh['blk'=4,'grp'=8] {'grp'}, dimensions={1}, use_global_device_ids=true | all-gather | bytes 73728 | tf_op jit(solution)/shard_map/all_gather | solution.py:53
  23.6 9.0 %all_gather.11 = bf16[32,32,128]{2,1,0:T(8,128)(2,1)S(1)} all-gather(bf16[8,32,128]{2,1,0:T(8,128)(2,1)S(1)} %copy.14), channel_id=1, replica_groups=mesh['blk'=4,'grp'=8] {'blk'}, dimensions={0}, use_global_device_ids=true | all-gather | bytes 327680 | tf_op jit(solution)/shard_map/all_gather | solution.py:70
  32.6 0.7 copy-done.5
  33.3 0.6 dynamic-slice
  34.5 0.6 copy-done.4
  35.3 7.3 %all-reduce = s32[32]{0:T(128)S(1)} all-reduce(s32[32]{0:T(128)S(1)} %dynamic-update-slice), channel_id=1, replica_groups=mesh['blk'=4,'grp'=8] {'blk'}, use_global_device_ids=true, to_apply=%add | all-reduce | flops 32 | bytes 256
  42.8 0.9 copy-done
  43.6 20.4 %while.20 = (s32[]{:T(128)}, f32[1024,128]{1,0:T(8,128)S(1)}, f32[]{:T(128)}, f32[256,4,128]{2,1,0:T(4,128)S(1)}, s32[32]{0:T(128)S(1)}, /*index=5*/s32[32]{0:T(...) while((s32[]{:T(128)}, f32[1024,128]{1,0:T(8,128)S(1)}, ...), condition=%wide.region_6.7_spmd.clone, body=%wide.region_0.6_spmd.clone.sunk | while | flops 207619808 | bytes 8279771 | solution.py:92
  43.7 0.7 iota_compare_fusion.3
  45.0 0.4 multiply_reduce_fusion.2
  45.8 0.7 fusion.33
  46.8 0.5 multiply_convert_fusion.2
  47.6 0.5 convolution_add_fusion.2
  48.7 0.7 iota_compare_fusion.3
  50.1 0.4 multiply_reduce_fusion.2
  50.9 0.7 fusion.33
  51.9 0.5 multiply_convert_fusion.2
  52.7 0.5 convolution_add_fusion.2
  53.8 0.7 iota_compare_fusion.3
  55.2 0.4 multiply_reduce_fusion.2
  56.0 0.7 fusion.33
  56.9 0.5 multiply_convert_fusion.2
  57.8 0.5 convolution_add_fusion.2
  58.9 0.7 iota_compare_fusion.3
  60.3 0.4 multiply_reduce_fusion.2
  61.1 0.7 fusion.33
  62.0 0.5 multiply_convert_fusion.2
  62.9 0.5 convolution_add_fusion.2
  64.0 0.8 copy-done.2
  64.8 129.3 %all-reduce.4.cloned.1.call-done = f32[256,4,128]{2,1,0:T(4,128)} async-done(((f32[256,4,128]{2,1,0:T(4,128)}), f32[256,4,128]{2,1,0:T(4,128)}) %all-reduce.4.cloned.1.call-update) | async-done | bytes 524304
  194.1 1.3 constant_dynamic-slice_fusion.1
  (63 shorter events, 6.9 us)
Async XLA Ops:
  7.2 187.0 %all-reduce.4.cloned.1.call-start = ((), (), s32[]{:S(2)}) async-start(), calls=%async_computation | async-start | bytes 1048576
  32.6 0.7 copy-start.5
  34.5 0.7 copy-start.4
  42.7 0.9 copy-start
  42.8 0.9 copy-start.3
  64.0 0.8 copy-start.2
  64.0 131.5 %copy-start.1 = (f32[1024,128]{1,0:T(8,128)}, f32[1024,128]{1,0:T(8,128)S(1)}, u32[]{:S(2)}) copy-start(f32[1024,128]{1,0:T(8,128)S(1)} %get-tuple-element.227) | copy-start | bytes 1572868
Sparse Core Ops, SparseCore 0:
  65.0 129.1 all-reduce.3
where the time goes:
time: 204 us; the launch traced here: 203 us
  waiting for transfers between devices  129 us (63%)
  blocking collectives  32 us (16%)
  between operations  15.9 us (8%)
  other arithmetic  11.7 us (6%)
  local copies, waits for them, and re-layouts  6.99 us (3%)
  matrix products  4.52 us (2%)
  loops' own time  2.95 us (1%)
    unnamed x2, waiting for transfers between devices  129 us
    all_gather x1, blocking collectives, local(): gathered = lax.all_gather(queries, 'grp', axis=1, tiled=True)  15.7 us
    all_gather x1, blocking collectives, local(): piece_queries = lax.all_gather(gathered, 'blk', axis=0, tiled=True)  8.99 us
    unnamed x1, blocking collectives  7.34 us
    unnamed x17, local copies, waits for them, and re-layouts  5.76 us
  transfers between devices with their start and end apart: 1, of which 1 were waited for; matrix products, arithmetic and copies ran while one was open for 0% of the time, Pallas kernels for 0%

commit v1 on v0

v1 whole, which is shorter than its diff:
```python
import functools
import math

import jax
import jax.numpy as jnp
from jax import lax
from jax.experimental import pallas as pl
from jax.experimental.pallas import tpu as pltpu
from jax.sharding import PartitionSpec as P

align_sharpness = 4.0
logit_scale = 2.0
logit_bias = -5.0
masked = -1e30
exp2_scale = align_sharpness * math.log2(math.e)
MESH = pl.DeviceIdType.MESH
patch_tile = 128


def partner(position, step, size):
    if size & (size - 1):
        return lax.rem(position + step, size)
    result = 0
    bit = 1
    while bit < size:
        here = lax.rem(position // bit, 2)
        flip = (step // bit) % 2
        result = result + (1 - here if flip else here) * bit
        bit *= 2
    return result


def source(position, step, size):
    if size & (size - 1):
        return lax.rem(position + size - step, size)
    return partner(position, step, size)


def fold(value):
    return value.reshape(-1, 8, value.shape[1])


def kernel(
    blocks, groups, block_queries, slice_tokens,
    query_ref, count_ref, page_ref, patch_count_ref, label_ref,
    query_grad_ref, page_grad_ref, loss_ref,
    held, count_rows, bias, scores, exponents, grads, own_term,
    part_send, part_recv, sum_send, sum_recv,
    column_send, column_recv, row_send, row_recv, count_send, count_recv,
    part_send_sem, part_recv_sem, sum_send_sem, sum_recv_sem,
):
    blk = lax.axis_index("blk")
    grp = lax.axis_index("grp")
    patches, width = page_ref.shape
    rows = block_queries * slice_tokens
    block_rows = rows * groups
    total_queries = blocks * block_queries
    tiles = [pl.ds(start, patch_tile) for start in range(0, patches, patch_tile)]

    barrier = pltpu.get_barrier_semaphore()
    for step in range(1, groups):
        pl.semaphore_signal(
            barrier, inc=1, device_id=(blk, partner(grp, step, groups)), device_id_type=MESH
        )
    for step in range(1, blocks):
        pl.semaphore_signal(
            barrier, inc=1, device_id=(partner(blk, step, blocks), grp), device_id_type=MESH
        )

    lane = lax.broadcasted_iota(jnp.int32, (1, block_rows), 1)
    query_row = lax.rem(lane // slice_tokens, block_queries)
    token_row = lane // rows * slice_tokens + lax.rem(lane, slice_tokens)
    counts = jnp.zeros((1, block_rows), jnp.float32)
    for index in range(block_queries):
        counts = jnp.where(query_row == index, count_ref[index].astype(jnp.float32), counts)
    count_rows[blk] = counts
    held[blk, grp] = query_ref[...]

    pl.semaphore_wait(barrier, groups - 1 + blocks - 1)

    def remote(src, dst, send, recv, device):
        pltpu.make_async_remote_copy(
            src_ref=src, dst_ref=dst, send_sem=send, recv_sem=recv,
            device_id=device, device_id_type=MESH,
        ).start()

    def settle(ref, sem):
        pltpu.make_async_copy(ref, ref, sem).wait()

    for step in range(groups - 1, 0, -1):
        remote(
            query_ref, held.at[blk, grp], column_send, column_recv.at[grp],
            (blk, partner(grp, step, groups)),
        )
    for step in range(1, blocks):
        other = partner(blk, step, blocks)
        remote(query_ref, held.at[blk, grp], row_send, row_recv.at[blk], (other, grp))
        remote(count_rows.at[blk], count_rows.at[blk], count_send, count_recv.at[blk], (other, grp))

    patch_count = patch_count_ref[0]
    for index, tile in enumerate(tiles):
        patch = index * patch_tile + lax.broadcasted_iota(jnp.int32, (patch_tile, width), 0)
        bias[tile, :] = jnp.where(patch < patch_count, 0.0, masked)
    same_query = (
        lax.rem(lax.broadcasted_iota(jnp.int32, (block_rows, block_rows), 0) // slice_tokens, block_queries)
        == lax.rem(lax.broadcasted_iota(jnp.int32, (block_rows, block_rows), 1) // slice_tokens, block_queries)
    )
    same_query = jnp.where(same_query, 1.0, 0.0).astype(jnp.bfloat16)

    for step in range(1, groups):
        origin = source(grp, step, groups)
        settle(held.at[blk, origin], column_recv.at[origin])
        for hop in range(1, blocks):
            remote(
                held.at[blk, origin], held.at[blk, origin], row_send, row_recv.at[blk],
                (partner(blk, hop, blocks), grp),
            )

    def block_terms(origin):
        query_rows = held[origin].reshape(block_rows, width)
        row_max = None
        for tile in tiles:
            tile_scores = lax.dot_general(
                page_ref[tile, :], query_rows, (((1,), (1,)), ((), ())),
                preferred_element_type=jnp.float32,
            )
            tile_bias = bias[tile, :]
            tile_scores = tile_scores + jnp.concatenate([tile_bias] * (block_rows // width), axis=1)
            scores[tile, :] = tile_scores
            tile_max = jnp.max(fold(tile_scores), axis=0)
            row_max = tile_max if row_max is None else jnp.maximum(row_max, tile_max)
        row_max = jnp.max(row_max, axis=0, keepdims=True)
        total = jnp.zeros((8, block_rows), jnp.float32)
        moment = jnp.zeros((8, block_rows), jnp.float32)
        for tile in tiles:
            shifted = scores[tile, :] - row_max
            exponent = jnp.exp2(shifted * exp2_scale)
            scores[tile, :] = shifted
            exponents[tile, :] = exponent
            total = total + jnp.sum(fold(exponent), axis=0)
            moment = moment + jnp.sum(fold(exponent * shifted), axis=0)
        total = jnp.sum(total, axis=0, keepdims=True)
        shifted_score = jnp.sum(moment, axis=0, keepdims=True) / total
        token_score = shifted_score + row_max

        count_row = count_rows[origin]
        live = token_row.astype(jnp.float32) < count_row
        remaining = jnp.where(live, token_score, 0.0)
        pieces = []
        for _ in range(3):
            piece = remaining.astype(jnp.bfloat16)
            pieces.append(piece)
            remaining = remaining - piece.astype(jnp.float32)
        pair_sum = sum(
            jnp.dot(
                jnp.broadcast_to(piece, (16, block_rows)), same_query,
                preferred_element_type=jnp.float32,
            )
            for piece in pieces
        )[0:1]
        pair_score = pair_sum / count_row
        label_row = jnp.zeros((1, block_rows), jnp.float32)
        for index in range(block_queries):
            label = label_ref[0, origin * block_queries + index].astype(jnp.float32)
            label_row = jnp.where(query_row == index, label, label_row)
        label_sign = 2.0 * label_row - 1.0
        signed = -label_sign * (logit_scale * pair_score + logit_bias)
        decay = jnp.exp(-jnp.abs(signed))
        softplus = jnp.maximum(signed, 0.0) + jnp.log1p(decay)
        sigmoid = jnp.where(signed >= 0.0, 1.0, decay) / (1.0 + decay)
        loss_row = jnp.where(token_row == 0, softplus, 0.0)
        token_grad = jnp.where(live, -label_sign * logit_scale * sigmoid / count_row, 0.0) / total
        slope = token_grad * align_sharpness
        offset = token_grad * (1.0 - align_sharpness * shifted_score)
        for tile in tiles:
            tile_grad = exponents[tile, :] * (offset + slope * scores[tile, :])
            grads[origin, tile, :] = tile_grad.astype(jnp.bfloat16)
        query_term = lax.dot_general(
            grads[origin], page_ref[...], (((0,), (0,)), ((), ())),
            preferred_element_type=jnp.float32,
        )
        return query_term, loss_row

    own, loss_row = block_terms(blk)
    own_term[...] = own.reshape(groups, rows, width)

    for step in range(1, blocks):
        origin = source(blk, step, blocks)
        settle(held.at[origin], row_recv.at[origin])
        settle(count_rows.at[origin], count_recv.at[origin])
        query_term, loss_term = block_terms(origin)
        loss_row = loss_row + loss_term
        part_send[origin] = query_term.astype(jnp.bfloat16).reshape(groups, rows, width)
        remote(
            part_send.at[origin], part_recv.at[blk], part_send_sem, part_recv_sem.at[blk],
            (origin, grp),
        )

    def page_term(tile):
        result = jnp.dot(
            grads[0, tile, :], held[0].reshape(block_rows, width), preferred_element_type=jnp.float32
        )
        for index in range(1, blocks):
            result = result + jnp.dot(
                grads[index, tile, :], held[index].reshape(block_rows, width),
                preferred_element_type=jnp.float32,
            )
        page_grad_ref[tile, :] = result

    half = len(tiles) // 2
    for tile in tiles[:half]:
        page_term(tile)

    block_sum = own_term[...]
    for step in range(1, blocks):
        origin = source(blk, step, blocks)
        settle(part_recv.at[origin], part_recv_sem.at[origin])
        block_sum = block_sum + part_recv[origin].astype(jnp.float32)
    own_term[...] = block_sum
    sum_send[...] = block_sum.astype(jnp.bfloat16)
    for step in range(groups - 1, 0, -1):
        target = partner(grp, step, groups)
        remote(
            sum_send.at[target], sum_recv.at[step - 1], sum_send_sem, sum_recv_sem, (blk, target)
        )
    for tile in tiles[half:]:
        page_term(tile)
    loss_ref[0] = jnp.sum(loss_row) / jnp.float32(total_queries)

    settle(sum_recv, sum_recv_sem)
    result = own_term[grp]
    for step in range(1, groups):
        result = result + sum_recv[step - 1].astype(jnp.float32)
    query_grad_ref[...] = result

    settle(held.at[0, pl.ds(0, groups - 1)], column_send)
    settle(held.at[pl.ds(0, blocks - 1)], row_send)
    settle(count_rows.at[pl.ds(0, blocks - 1)], count_send)
    settle(part_send.at[pl.ds(0, blocks - 1)], part_send_sem)
    settle(sum_send.at[pl.ds(0, groups - 1)], sum_send_sem)


def local(queries, token_counts, pages, patch_counts, labels):
    blocks = lax.axis_size("blk")
    groups = lax.axis_size("grp")
    block_queries, slice_tokens, width = queries.shape
    patches = pages.shape[1]
    rows = block_queries * slice_tokens
    block_rows = rows * groups
    vmem = pl.BlockSpec(memory_space=pltpu.VMEM)
    smem = pl.BlockSpec(memory_space=pltpu.SMEM)
    dma = pltpu.SemaphoreType.DMA
    query_grad, page_grad, page_loss = pl.pallas_call(
        functools.partial(kernel, blocks, groups, block_queries, slice_tokens),
        out_shape=(
            jax.ShapeDtypeStruct((rows, width), jnp.float32),
            jax.ShapeDtypeStruct((patches, width), jnp.float32),
            jax.ShapeDtypeStruct((1,), jnp.float32),
        ),
        in_specs=[vmem, smem, vmem, smem, smem],
        out_specs=(vmem, vmem, smem),
        scratch_shapes=[
            pltpu.VMEM((blocks, groups, rows, width), jnp.bfloat16),
            pltpu.VMEM((blocks, 1, block_rows), jnp.float32),
            pltpu.VMEM((patches, width), jnp.float32),
            pltpu.VMEM((patches, block_rows), jnp.float32),
            pltpu.VMEM((patches, block_rows), jnp.float32),
            pltpu.VMEM((blocks, patches, block_rows), jnp.bfloat16),
            pltpu.VMEM((groups, rows, width), jnp.float32),
            pltpu.VMEM((blocks, groups, rows, width), jnp.bfloat16),
            pltpu.VMEM((blocks, groups, rows, width), jnp.bfloat16),
            pltpu.VMEM((groups, rows, width), jnp.bfloat16),
            pltpu.VMEM((groups - 1, rows, width), jnp.bfloat16),
            dma, dma((groups,)), dma, dma((blocks,)), dma, dma((blocks,)),
            dma, dma((blocks,)), dma, dma,
        ],
        compiler_params=pltpu.CompilerParams(
            collective_id=0, has_side_effects=True, vmem_limit_bytes=60 * 1024 * 1024
        ),
        name="late_interaction",
    )(queries.reshape(rows, width), token_counts, pages[0], patch_counts, labels.T)
    return query_grad.reshape(queries.shape), page_grad[None], page_loss


def solution(mesh):
    in_specs = (
        P("blk", "grp", None),
        P("blk"),
        P(("blk", "grp"), None, None),
        P(("blk", "grp")),
        P(None, ("blk", "grp")),
    )
    out_specs = (P("blk", "grp", None), P(("blk", "grp"), None, None), P(("blk", "grp")))
    return jax.shard_map(local, mesh=mesh, in_specs=in_specs, out_specs=out_specs, check_vma=False)
```

time: 204 us -> 32.4 us (0.16)
  waiting for transfers between devices: 129 us -> 0 us
  blocking collectives: 32 us -> 0 us
  Pallas kernels: 0 us -> 25.8 us
  between operations: 15.9 us -> 3.05 us
  other arithmetic: 11.7 us -> 0 us
  matrix products: 4.52 us -> 0 us
  local copies, waits for them, and re-layouts: 6.99 us -> 3.19 us
  loops' own time: 2.95 us -> 0 us
    unnamed x2 -> x0, waiting for transfers between devices: 129 us -> none
    pallas_call x0 -> x1, Pallas kernels: none -> 25.8 us  [local(): pl.pallas_call(functools.partial(kernel, blocks, groups, block_queries, s...]
    all_gather x2 -> x0, blocking collectives: 24.7 us -> none  [the longest x1 15.7 us: local(): gathered = lax.all_gather(queries, 'grp', axis=1, tiled=True)]
    unnamed x1 -> x0, blocking collectives: 7.34 us -> none
    reduce_sum x16 -> x0, other arithmetic: 6.68 us -> none  [the longest x4 2.84 us: align(): loss_sum = jnp.sum(jax.nn.softplus(-label_sign * pair_logit))]
    dot_general x12 -> x0, matrix products: 4.52 us -> none  [the longest x4 1.84 us: align(): jnp.dot(scores_grad.T, query_rows, preferred_element_type=jnp.float32)]
    another operation x1 -> x0, loops' own time: 2.95 us -> none  [local(): lax.fori_loop(0, count_blocks, one_block, (empty_page, jnp.float32(0.0),...]
    lt x4 -> x0, other arithmetic: 2.61 us -> none  [align(): patch_mask = jnp.arange(page_rows.shape[0]) < patch_count]
  transfers between devices with their start and end apart: 1 -> 0, of which waited for: 1 -> 0; matrix products, arithmetic and copies ran while one was open for 0% -> 0% of each run, Pallas kernels for 0% -> 0%
where the time goes in v1:
time: 32.4 us; the launch traced here: 32 us
  Pallas kernels  25.8 us (80%)
  local copies, waits for them, and re-layouts  3.19 us (10%)
  between operations  3.05 us (9%)
    pallas_call x1, Pallas kernels, local(): pl.pallas_call(functools.partial(kernel, blocks, groups, block_queries, s...  25.8 us
    unnamed x2, local copies, waits for them, and re-layouts  3.19 us

profile of v1, /device:TPU:0, one launch (start us, length us, event | category | flops | bytes accessed | tf_op | source)
XLA Modules:
  0.0 32.0 jit_solution(10259918748577312298)
XLA Ops:
  1.3 25.8 %late_interaction.1 = (f32[32,128]{1,0:T(8,128)}, f32[1024,128]{1,0:T(8,128)}, f32[1]{0:T(128)}) custom-call(bf16[32,128]{1,0:T(8,128)(2,1)} %bitcast.8, s32[8]{0:T(128)} %count_ref.1, bf16[1024,128]{1,0:T(8,128)(2,1)} %bitcast.6, s32[1]{0:T(128)S(6)} %copy.11.patch_count_ref, s32[1,32]{1,0:T(1,128)} %bitcast.9), custom_call_target="tpu_custom_call" | custom-call | tf_op jit(solution)/shard_map/late_interaction/pallas_call | solution.py:253
  27.1 1.3 %copy.12 = f32[8,4,128]{2,1,0:T(4,128)} copy(f32[8,4,128]{2,1,0:T(4,128)} %bitcast.7) | data formatting | bytes 32768
  28.4 1.9 %copy.13 = f32[1,1024,128]{2,1,0:T(8,128)} copy(f32[1,1024,128]{2,1,0:T(8,128)} %bitcast.5) | data formatting | bytes 1048576

commit v2 on v1

--- a/solution.py
+++ b/solution.py
@@ -42,12 +42,13 @@
 
 def kernel(
     blocks, groups, block_queries, slice_tokens,
+    query_in, count_in, page_in, patch_count_in, label_in,
+    query_grad_ref, page_grad_ref, loss_ref,
     query_ref, count_ref, page_ref, patch_count_ref, label_ref,
-    query_grad_ref, page_grad_ref, loss_ref,
     held, count_rows, bias, scores, exponents, grads, own_term,
     part_send, part_recv, sum_send, sum_recv,
     column_send, column_recv, row_send, row_recv, count_send, count_recv,
-    part_send_sem, part_recv_sem, sum_send_sem, sum_recv_sem,
+    part_send_sem, part_recv_sem, sum_send_sem, sum_recv_sem, load_sem,
 ):
     blk = lax.axis_index("blk")
     grp = lax.axis_index("grp")
@@ -62,14 +63,26 @@
         pl.semaphore_signal(
             barrier, inc=1, device_id=(blk, partner(grp, step, groups)), device_id_type=MESH
         )
-    for step in range(1, blocks):
+    for step in range(blocks - 1, 0, -1):
         pl.semaphore_signal(
             barrier, inc=1, device_id=(partner(blk, step, blocks), grp), device_id_type=MESH
         )
+
+    loads = [
+        pltpu.make_async_copy(src, dst, load_sem.at[index])
+        for index, (src, dst) in enumerate((
+            (query_in, query_ref), (count_in, count_ref), (page_in, page_ref),
+            (patch_count_in, patch_count_ref), (label_in, label_ref),
+        ))
+    ]
+    for load in loads:
+        load.start()
 
     lane = lax.broadcasted_iota(jnp.int32, (1, block_rows), 1)
     query_row = lax.rem(lane // slice_tokens, block_queries)
     token_row = lane // rows * slice_tokens + lax.rem(lane, slice_tokens)
+    loads[0].wait()
+    loads[1].wait()
     counts = jnp.zeros((1, block_rows), jnp.float32)
     for index in range(block_queries):
         counts = jnp.where(query_row == index, count_ref[index].astype(jnp.float32), counts)
@@ -92,11 +105,13 @@
             query_ref, held.at[blk, grp], column_send, column_recv.at[grp],
             (blk, partner(grp, step, groups)),
         )
-    for step in range(1, blocks):
+    for step in range(blocks - 1, 0, -1):
         other = partner(blk, step, blocks)
         remote(query_ref, held.at[blk, grp], row_send, row_recv.at[blk], (other, grp))
         remote(count_rows.at[blk], count_rows.at[blk], count_send, count_recv.at[blk], (other, grp))
 
+    for load in loads[2:]:
+        load.wait()
     patch_count = patch_count_ref[0]
     for index, tile in enumerate(tiles):
         patch = index * patch_tile + lax.broadcasted_iota(jnp.int32, (patch_tile, width), 0)
@@ -110,7 +125,7 @@
     for step in range(1, groups):
         origin = source(grp, step, groups)
         settle(held.at[blk, origin], column_recv.at[origin])
-        for hop in range(1, blocks):
+        for hop in range(blocks - 1, 0, -1):
             remote(
                 held.at[blk, origin], held.at[blk, origin], row_send, row_recv.at[blk],
                 (partner(blk, hop, blocks), grp),
@@ -184,7 +199,7 @@
     own, loss_row = block_terms(blk)
     own_term[...] = own.reshape(groups, rows, width)
 
-    for step in range(1, blocks):
+    for step in range(blocks - 1, 0, -1):
         origin = source(blk, step, blocks)
         settle(held.at[origin], row_recv.at[origin])
         settle(count_rows.at[origin], count_recv.at[origin])
@@ -212,7 +227,7 @@
         page_term(tile)
 
     block_sum = own_term[...]
-    for step in range(1, blocks):
+    for step in range(blocks - 1, 0, -1):
         origin = source(blk, step, blocks)
         settle(part_recv.at[origin], part_recv_sem.at[origin])
         block_sum = block_sum + part_recv[origin].astype(jnp.float32)
@@ -240,6 +255,18 @@
     settle(sum_send.at[pl.ds(0, groups - 1)], sum_send_sem)
 
 
+def write_out(query_grad_in, page_grad_in, loss_in, query_grad_ref, page_grad_ref, loss_ref, sems):
+    copies = [
+        pltpu.make_async_copy(page_grad_in, page_grad_ref, sems.at[0]),
+        pltpu.make_async_copy(query_grad_in, query_grad_ref, sems.at[1]),
+        pltpu.make_async_copy(loss_in, loss_ref, sems.at[2]),
+    ]
+    for copy in copies:
+        copy.start()
+    for copy in copies:
+        copy.wait()
+
+
 def local(queries, token_counts, pages, patch_counts, labels):
     blocks = lax.axis_size("blk")
     groups = lax.axis_size("grp")
@@ -249,17 +276,23 @@
     block_rows = rows * groups
     vmem = pl.BlockSpec(memory_space=pltpu.VMEM)
     smem = pl.BlockSpec(memory_space=pltpu.SMEM)
+    anywhere = pl.BlockSpec(memory_space=pl.ANY)
     dma = pltpu.SemaphoreType.DMA
     query_grad, page_grad, page_loss = pl.pallas_call(
         functools.partial(kernel, blocks, groups, block_queries, slice_tokens),
         out_shape=(
-            jax.ShapeDtypeStruct((rows, width), jnp.float32),
-            jax.ShapeDtypeStruct((patches, width), jnp.float32),
-            jax.ShapeDtypeStruct((1,), jnp.float32),
+            pltpu.VMEM((rows, width), jnp.float32),
+            pltpu.VMEM((patches, width), jnp.float32),
+            pltpu.SMEM((1,), jnp.float32),
         ),
-        in_specs=[vmem, smem, vmem, smem, smem],
+        in_specs=[anywhere] * 5,
         out_specs=(vmem, vmem, smem),
         scratch_shapes=[
+            pltpu.VMEM((rows, width), jnp.bfloat16),
+            pltpu.SMEM(token_counts.shape, jnp.int32),
+            pltpu.VMEM((patches, width), jnp.bfloat16),
+            pltpu.SMEM((1,), jnp.int32),
+            pltpu.SMEM((1, labels.shape[0]), jnp.int32),
             pltpu.VMEM((blocks, groups, rows, width), jnp.bfloat16),
             pltpu.VMEM((blocks, 1, block_rows), jnp.float32),
             pltpu.VMEM((patches, width), jnp.float32),
@@ -272,13 +305,26 @@
             pltpu.VMEM((groups, rows, width), jnp.bfloat16),
             pltpu.VMEM((groups - 1, rows, width), jnp.bfloat16),
             dma, dma((groups,)), dma, dma((blocks,)), dma, dma((blocks,)),
-            dma, dma((blocks,)), dma, dma,
+            dma, dma((blocks,)), dma, dma, dma((5,)),
         ],
         compiler_params=pltpu.CompilerParams(
             collective_id=0, has_side_effects=True, vmem_limit_bytes=60 * 1024 * 1024
         ),
         name="late_interaction",
     )(queries.reshape(rows, width), token_counts, pages[0], patch_counts, labels.T)
+    query_grad, page_grad, page_loss = pl.pallas_call(
+        write_out,
+        out_shape=(
+            jax.ShapeDtypeStruct((rows, width), jnp.float32),
+            jax.ShapeDtypeStruct((patches, width), jnp.float32),
+            jax.ShapeDtypeStruct((1,), jnp.float32),
+        ),
+        in_specs=[anywhere] * 3,
+        out_specs=(anywhere,) * 3,
+        scratch_shapes=[dma((3,))],
+        compiler_params=pltpu.CompilerParams(vmem_limit_bytes=1024 * 1024),
+        name="write_out",
+    )(query_grad, page_grad, page_loss)
     return query_grad.reshape(queries.shape), page_grad[None], page_loss
 
 

time: 32.4 us -> 26.4 us (0.81)
  local copies, waits for them, and re-layouts: 3.19 us -> 0 us
  between operations: 3.05 us -> 1.29 us
  Pallas kernels: 25.8 us -> 24.9 us
    unnamed x2 -> x0, local copies, waits for them, and re-layouts: 3.19 us -> none
    pallas_call x1, Pallas kernels: 25.8 us -> 24.1 us  [local(): pl.pallas_call(functools.partial(kernel, blocks, groups, block_queries, s...]
    pallas_call x0 -> x1, Pallas kernels: none -> 0.83 us  [local(): pl.pallas_call(write_out, out_shape=(jax.ShapeDtypeStruct((rows, width),...]
where the time goes in v2:
time: 26.4 us; the launch traced here: 26.2 us
  Pallas kernels  24.9 us (94%)
  between operations  1.29 us (5%)
    pallas_call x1, Pallas kernels, local(): pl.pallas_call(functools.partial(kernel, blocks, groups, block_queries, s...  24.1 us
    pallas_call x1, Pallas kernels, local(): pl.pallas_call(write_out, out_shape=(jax.ShapeDtypeStruct((rows, width),...  0.83 us

profile of v2, /device:TPU:0, one launch (start us, length us, event | category | flops | bytes accessed | tf_op | source)
XLA Modules:
  0.0 26.2 jit_solution(6049601702844358219)
XLA Ops:
  1.3 24.1 %late_interaction.1 = (f32[32,128]{1,0:T(8,128)S(1)}, f32[1024,128]{1,0:T(8,128)S(1)}, f32[1]{0:T(128)S(4)}) custom-call(bf16[32,128]{1,0:T(8,128)(2,1)} %bitcast.6, s32[8]{0:T(128)} %count_in.1, bf16[1024,128]{1,0:T(8,128)(2,1)} %bitcast.5, s32[1]{0:T(128)S(6)} %copy.8.patch_count_in, s32[1,32]{1,0:T(1,128)} %bitcast.7), custom_call_target="tpu_custom_call" | custom-call | tf_op jit(solution)/shard_map/late_interaction/pallas_call | solution.py:281
  25.3 0.8 %write_out.1 = (f32[32,128]{1,0:T(8,128)}, f32[1024,128]{1,0:T(8,128)}, f32[1]{0:T(128)}) custom-call(f32[32,128]{1,0:T(8,128)S(1)} %get-tuple-element.9.query_grad_in, f32[1024,128]{1,0:T(8,128)S(1)} %get-tuple-element.10.page_grad_in, f32[1]{0:T(128)S(4)} %get-tuple-element.11.loss_in), custom_call_target="tpu_custom_call" | custom-call | tf_op jit(solution)/shard_map/write_out/pallas_call | solution.py:315

commit v3 on v2

--- a/solution.py
+++ b/solution.py
@@ -161,18 +161,18 @@
         count_row = count_rows[origin]
         live = token_row.astype(jnp.float32) < count_row
         remaining = jnp.where(live, token_score, 0.0)
-        pieces = []
-        for _ in range(3):
-            piece = remaining.astype(jnp.bfloat16)
-            pieces.append(piece)
-            remaining = remaining - piece.astype(jnp.float32)
-        pair_sum = sum(
+        sublane = lax.broadcasted_iota(jnp.int32, (16, block_rows), 0)
+        pieces = jnp.zeros((16, block_rows), jnp.float32)
+        for index in range(3):
+            piece = remaining.astype(jnp.bfloat16).astype(jnp.float32)
+            pieces = jnp.where(sublane == index, piece, pieces)
+            remaining = remaining - piece
+        pair_sum = jnp.sum(
             jnp.dot(
-                jnp.broadcast_to(piece, (16, block_rows)), same_query,
-                preferred_element_type=jnp.float32,
-            )
-            for piece in pieces
-        )[0:1]
+                pieces.astype(jnp.bfloat16), same_query, preferred_element_type=jnp.float32
+            ),
+            axis=0, keepdims=True,
+        )
         pair_score = pair_sum / count_row
         label_row = jnp.zeros((1, block_rows), jnp.float32)
         for index in range(block_queries):

time: 26.4 us -> 26 us (0.985)
  Pallas kernels: 24.9 us -> 24.5 us
    pallas_call x1, Pallas kernels: 24.1 us -> 23.7 us  [local(): pl.pallas_call(functools.partial(kernel, blocks, groups, block_queries, s...]
where the time goes in v3:
time: 26 us; the launch traced here: 25.8 us
  Pallas kernels  24.5 us (94%)
  between operations  1.29 us (5%)
    pallas_call x1, Pallas kernels, local(): pl.pallas_call(functools.partial(kernel, blocks, groups, block_queries, s...  23.7 us
    pallas_call x1, Pallas kernels, local(): pl.pallas_call(write_out, out_shape=(jax.ShapeDtypeStruct((rows, width),...  0.83 us

profile of v3, /device:TPU:0, one launch (start us, length us, event | category | flops | bytes accessed | tf_op | source)
XLA Modules:
  0.0 25.8 jit_solution(5467220532268101644)
XLA Ops:
  1.3 23.7 %late_interaction.1 = (f32[32,128]{1,0:T(8,128)S(1)}, f32[1024,128]{1,0:T(8,128)S(1)}, f32[1]{0:T(128)S(4)}) custom-call(bf16[32,128]{1,0:T(8,128)(2,1)} %bitcast.6, s32[8]{0:T(128)} %count_in.1, bf16[1024,128]{1,0:T(8,128)(2,1)} %bitcast.5, s32[1]{0:T(128)S(6)} %copy.8.patch_count_in, s32[1,32]{1,0:T(1,128)} %bitcast.7), custom_call_target="tpu_custom_call" | custom-call | tf_op jit(solution)/shard_map/late_interaction/pallas_call | solution.py:281
  25.0 0.8 %write_out.1 = (f32[32,128]{1,0:T(8,128)}, f32[1024,128]{1,0:T(8,128)}, f32[1]{0:T(128)}) custom-call(f32[32,128]{1,0:T(8,128)S(1)} %get-tuple-element.9.query_grad_in, f32[1024,128]{1,0:T(8,128)S(1)} %get-tuple-element.10.page_grad_in, f32[1]{0:T(128)S(4)} %get-tuple-element.11.loss_in), custom_call_target="tpu_custom_call" | custom-call | tf_op jit(solution)/shard_map/write_out/pallas_call | solution.py:315
